TPU v7x, 256 devices: a whole 4x4x8 slice. The times are simulated.
256 devices in a mesh: gx: 4 (over x), gy: 4 (over y_lo, core), gz: 16 (over z, y_hi).
Axes of the slice: x: 4, y: 4 (y_hi: 2, y_lo: 2; y = y_hi * 2 + y_lo), z: 8, core: 2. Of those that a mesh axis runs over, the one named last changes fastest.
Arguments:
- left_modes: bfloat16 [2, 4, 2, 128, 3, 131072], P(None, None, None, None, None, ('gx', 'gy', 'gz')), may hold values from -0.14160156 to 0.14160156
- right_modes: bfloat16 [2, 4, 2, 128, 3, 131072], P(None, None, None, None, None, ('gx', 'gy', 'gz')), may hold values from -0.14160156 to 0.14160156
- gamma_cols: int32 [16, 4], replicated, may hold values from 0 to 3, each once within a row
- gamma_phase: int32 [16, 4], replicated, may hold values from 0 to 3
- dilution: int32 [64], replicated, may hold values from 0 to 3
- time_pairs: int32 [4, 2], replicated, may hold values from 0 to 1
Outputs:
- meson_fields: float32 [16, 2, 2, 128, 128], P('gz', None, None, ('gx', 'gy'))
- traces: float32 [4, 16, 16, 2], P(None, 'gz')
Inputs may be any that keep to these rules, and one draw needn't show every extreme that they name: Each row of gamma_cols is a permutation of the four spins.
All inputs are finite; a program needn't handle non-finite values.
Results may differ from a plain program's by a relative error of at most 0.0003.
Values sent between devices are 32-bit elements; how exact they have to be, the bound alone decides.
No kernel may reach another device: no remote copies, remote signals or barrier semaphores. Data moves between devices by JAX's collectives and lax.ppermute only.
A program may use at most 128 MiB of HBM per device.

v0:
```python
import jax
import jax.numpy as jnp
from jax import lax
from jax.sharding import PartitionSpec as P

EXACT = lax.Precision.HIGHEST


def coefficients(gamma_cols, gamma_phase):
    spin_ids = jnp.arange(4, dtype=jnp.int32)
    onehot = (gamma_cols[:, :, None] == spin_ids[None, None, :]).astype(jnp.float32)
    real_sign = (gamma_phase == 0).astype(jnp.float32) - (gamma_phase == 2).astype(jnp.float32)
    imag_sign = (gamma_phase == 1).astype(jnp.float32) - (gamma_phase == 3).astype(jnp.float32)
    return (onehot * real_sign[:, :, None], onehot * imag_sign[:, :, None])


def select_pairs(crossed, time_pairs):
    time_ids = jnp.arange(crossed.shape[1], dtype=jnp.int32)
    first_time = (time_pairs[:, 0:1] == time_ids[None, :]).astype(jnp.float32)
    second_time = (time_pairs[:, 1:2] == time_ids[None, :]).astype(jnp.float32)
    chosen = jnp.einsum("pt,pu,gtahub->pgahb", first_time, second_time, crossed, precision=EXACT)
    real_part = chosen[:, :, 0, :, 0] - chosen[:, :, 1, :, 1]
    imag_part = chosen[:, :, 0, :, 1] + chosen[:, :, 1, :, 0]
    return jnp.stack([real_part, imag_part], axis=-1)


def project(coef_re, coef_im, pair_re, pair_im, form, part_axis):
    meson_re = jnp.einsum(form, coef_re, pair_re, precision=EXACT) - jnp.einsum(
        form, coef_im, pair_im, precision=EXACT
    )
    meson_im = jnp.einsum(form, coef_re, pair_im, precision=EXACT) + jnp.einsum(
        form, coef_im, pair_re, precision=EXACT
    )
    return jnp.stack([meson_re, meson_im], axis=part_axis)


def finish_whole(summed, time_pairs, local_gammas, block_rows, mode_count):
    group_start = lax.axis_index("gz") * local_gammas
    my_gammas = lax.dynamic_slice_in_dim(summed, group_start, local_gammas, 0)
    row_block = lax.axis_index("gx") * lax.axis_size("gy") + lax.axis_index("gy")
    meson_fields = lax.dynamic_slice_in_dim(my_gammas, row_block * block_rows, block_rows, 3)
    crossed = jnp.einsum("gtaij,hubji->gtahub", my_gammas, summed, precision=EXACT)
    traces = select_pairs(crossed, time_pairs) / mode_count
    return (meson_fields, traces)


def local(left_modes, right_modes, gamma_cols, gamma_phase, dilution, time_pairs):
    times_held = left_modes.shape[0]
    mode_count = left_modes.shape[3]
    gamma_count = gamma_cols.shape[0]
    noise_count = dilution.shape[0]
    low_count = mode_count - noise_count
    coef_re, coef_im = coefficients(gamma_cols, gamma_phase)
    groups = lax.axis_size("gz")
    blocks = lax.axis_size("gx") * lax.axis_size("gy")
    local_gammas = gamma_count // groups
    block_rows = mode_count // blocks
    spin_ids = jnp.arange(4, dtype=jnp.int32)
    noise_onehot = dilution[None, :] == spin_ids[:, None]
    select_table = noise_onehot.astype(jnp.bfloat16)
    low_re_list = []
    low_im_list = []
    noise_re_list = []
    noise_im_list = []
    for time_slot in range(times_held):
        left_slot = left_modes[time_slot]
        right_slot = right_modes[time_slot]
        low_prod = jnp.einsum(
            "spicx,qrjcx->sqpirj",
            left_slot,
            right_slot[:, :, :low_count],
            preferred_element_type=jnp.float32,
        )
        noise_right = jnp.sum(
            right_slot[:, :, low_count:] * select_table[:, None, :, None, None], axis=0
        )
        noise_prod = jnp.einsum(
            "spicx,qjcx->spiqj", left_slot, noise_right, preferred_element_type=jnp.float32
        )
        low_re_list.append(low_prod[:, :, 0, :, 0, :] + low_prod[:, :, 1, :, 1, :])
        low_im_list.append(low_prod[:, :, 0, :, 1, :] - low_prod[:, :, 1, :, 0, :])
        noise_re_list.append(noise_prod[:, 0, :, 0, :] + noise_prod[:, 1, :, 1, :])
        noise_im_list.append(noise_prod[:, 0, :, 1, :] - noise_prod[:, 1, :, 0, :])
    low_re, low_im, noise_re, noise_im = lax.psum(
        (
            jnp.stack(low_re_list),
            jnp.stack(low_im_list),
            jnp.stack(noise_re_list),
            jnp.stack(noise_im_list),
        ),
        ("gx", "gy", "gz"),
    )
    noise_float = noise_onehot.astype(jnp.float32)
    noise_coef_re = jnp.einsum("gsr,rj->gsj", coef_re, noise_float, precision=EXACT)
    noise_coef_im = jnp.einsum("gsr,rj->gsj", coef_im, noise_float, precision=EXACT)
    low_part = project(coef_re, coef_im, low_re, low_im, "gsr,tsrij->gtij", 2)
    noise_part = project(noise_coef_re, noise_coef_im, noise_re, noise_im, "gsj,tsij->gtij", 2)
    summed = jnp.concatenate([low_part, noise_part], axis=4)
    meson_fields, traces = finish_whole(summed, time_pairs, local_gammas, block_rows, mode_count)
    return (meson_fields, traces)


def solution(mesh):
    return jax.shard_map(
        local,
        mesh=mesh,
        in_specs=(
            P(None, None, None, None, None, ("gx", "gy", "gz")),
            P(None, None, None, None, None, ("gx", "gy", "gz")),
            P(),
            P(),
            P(),
            P(),
        ),
        out_specs=(P("gz", None, None, ("gx", "gy"), None), P(None, "gz", None, None)),
        check_vma=False,
    )
```

profile of v0, /device:TPU:2, one launch (start us, length us, event | category | flops | bytes accessed | tf_op | source)
XLA Modules:
  0.0 340.3 jit_solution(10529417758410979270)
XLA Ops:
  7.2 0.0 copy-start.7
  7.2 0.0 all-reduce.3.cloned.1.call-start
  7.2 0.0 copy-start.3
  7.2 3.5 %slice_bitcast_fusion = (bf16[4,2,128,3,512]{4,2,3,1,0:T(8,128)(2,1)S(1)}, bf16[4,2,128,3,512]{4,2,3,1,0:T(8,128)(2,1)S(1)}) fusion(bf16[2,4,2,128,3,512]{5,3,4,2,1,0:T(8,128)(2,1)} %param.7), kind=kLoop, calls=%fused_computation.11 | loop fusion | bytes 12582912 | tf_op jit(solution)/shard_map/squeeze | solution.py:67
  10.7 0.0 copy-done.7
  10.7 1.1 copy-done.3
  11.9 0.7 slice_bitcast_fusion.3
  12.6 0.9 fusion.19
  13.5 1.1 fusion.30
  14.7 1.8 fusion.15
  16.5 0.1 fusion.38
  16.6 0.1 fusion.41
  16.7 1.1 fusion.27
  17.8 1.8 fusion.12
  19.6 0.1 fusion.37
  19.8 0.8 pad_maximum_fusion.2
  20.6 0.0 copy-start.8
  20.6 0.0 copy-start.6
  20.6 0.0 copy-start.9
  20.6 1.5 pad_maximum_fusion
  22.1 0.0 all-reduce.3.cloned.1.call-update
  22.2 0.0 copy-done.8
  22.2 0.0 copy-done.6
  22.2 0.2 fusion.61
  22.4 0.1 copy.23
  22.5 0.2 fusion.59
  22.8 0.1 copy.25
  22.9 0.0 copy-done.9
  22.9 268.4 %all-reduce.3.cloned.1.call-done = (f32[2,4,128,64]{2,3,1,0:T(8,128)}, f32[2,4,128,64]{2,3,1,0:T(8,128)}, f32[2,4,4,128,64]{3,4,1,2,0:T(8,128)}, f32[2,4,4,128,64]{3,4,1,2,0:T(8,128)}) async-done(((f32[2,4,128,64]{2,3,1,0:T(8,128)}, f32[2,4,128,64]{2,3,1,0:T(8,128)}, f32[2,4,4,128,64]{3,4,1,2,0:T(8,128)}, f32[2,4,4,128,64]{3,4,1,2,0:T(8,128)}), (f32[2,4,128,64]{2,3,1,0:T(8,128)}, ...) | async-done | bytes 2621456 | tf_op jit(solution)/shard_map/psum | solution.py:84
  291.3 0.0 copy-start.2
  291.3 3.3 convolution_bitcast_fusion.2
  294.6 0.0 copy-start.1
  294.6 3.3 convolution_bitcast_fusion
  297.9 0.0 copy-done.2
  298.0 0.0 copy-start.4
  298.0 0.0 copy-start.5
  298.0 2.0 fusion.24
  300.0 0.0 copy-done.1
  300.0 2.2 fusion.26
  302.2 0.0 copy-done.4
  302.2 1.2 fusion.48
  303.4 0.0 copy-done.5
  303.4 1.2 fusion.44
  304.5 1.2 fusion.22
  305.7 1.2 fusion.21
  306.9 2.7 fusion.101
  309.6 0.0 copy-start
  309.6 2.0 copy-done
  311.6 0.2 constant_dynamic-slice_fusion
  311.7 0.2 copy.67
  311.9 17.7 %fusion = f32[2,2,16,2,2,1]{2,1,5,4,3,0:T(2,128)S(1)} fusion(f32[2,2,128,128,1,1]{3,1,2,5,4,0:T(2,128)S(1)} %copy.67, f32[16,2,2,128,128,1]{3,0,4,1,2,5:T(8,128)} %get-tuple-element.14), kind=kOutput, calls=%fused_computation.1 | convolution fusion | flops 50331648 | bytes 4457472 | tf_op jit(solution)/shard_map/gtaij,hubji->gtahub/dot_general | solution.py:42
  329.7 0.2 convolution_bitcast_fusion.4
  329.9 0.6 copy.35
  330.5 2.2 constant_dynamic-slice_fusion.1
  332.7 0.7 copy.34
  (9 shorter events, 0.1 us)
Async XLA Ops:
  7.2 3.6 %copy-start.7 = (s32[64]{0:T(128)S(1)}, s32[64]{0:T(128)}, u32[]{:S(2)}) copy-start(s32[64]{0:T(128)} %param.10) | copy-start | bytes 772
  7.2 284.1 %all-reduce.3.cloned.1.call-start = ((), (), s32[]{:S(2)}) async-start(), calls=%async_computation | async-start | bytes 5242880 | tf_op jit(solution)/shard_map/psum | solution.py:84
  7.2 4.6 %copy-start.3 = (bf16[2,4,2,128,3,512]{5,3,4,2,1,0:T(8,128)(2,1)S(1)}, bf16[2,4,2,128,3,512]{5,3,4,2,1,0:T(8,128)(2,1)}, u32[]{:S(2)}) copy-start(bf16[2,4,2,128,3,512]{5,3,4,2,1,0:T(8,128)(2,1)} %param.6) | copy-start | bytes 18874372
  20.6 1.5 copy-start.8
  20.6 1.6 copy-start.6
  20.6 2.3 copy-start.9
  291.3 6.6 %copy-start.2 = (f32[2,4,4,128,64]{3,4,1,2,0:T(8,128)S(1)}, f32[2,4,4,128,64]{3,4,1,2,0:T(8,128)}, u32[]{:S(2)}) copy-start(f32[2,4,4,128,64]{3,4,1,2,0:T(8,128)} %get-tuple-element.8) | copy-start | bytes 3145732
  294.6 5.4 %copy-start.1 = (f32[2,4,4,128,64]{3,4,1,2,0:T(8,128)S(1)}, f32[2,4,4,128,64]{3,4,1,2,0:T(8,128)}, u32[]{:S(2)}) copy-start(f32[2,4,4,128,64]{3,4,1,2,0:T(8,128)} %get-tuple-element.9) | copy-start | bytes 3145732
  298.0 4.2 %copy-start.4 = (f32[2,4,128,64]{2,3,1,0:T(8,128)S(1)}, f32[2,4,128,64]{2,3,1,0:T(8,128)}, u32[]{:S(2)}) copy-start(f32[2,4,128,64]{2,3,1,0:T(8,128)} %get-tuple-element.7) | copy-start | bytes 786436
  298.0 5.4 %copy-start.5 = (f32[2,4,128,64]{2,3,1,0:T(8,128)S(1)}, f32[2,4,128,64]{2,3,1,0:T(8,128)}, u32[]{:S(2)}) copy-start(f32[2,4,128,64]{2,3,1,0:T(8,128)} %get-tuple-element.6) | copy-start | bytes 786436
  309.6 2.0 copy-start
Sparse Core Ops, SparseCore 0:
  22.3 268.9 all-reduce.2
where the time goes:
time: 340 us
  waiting for transfers between devices  268 us (79%)
  matrix products  39.7 us (12%)
  between operations  14.4 us (4%)
  local copies, waits for them, and re-layouts  11.4 us (3%)
  other arithmetic  6.28 us (2%)
    psum x1, waiting for transfers between devices, local(): lax.psum((jnp.stack(low_re_list), jnp.stack(low_im_list), jnp.stack(noise...  268 us
    dot_general x1, matrix products, finish_whole(): jnp.einsum('gtaij,hubji->gtahub', my_gammas, summed, precision=EXACT)  17.7 us
  transfers between devices with their start and end apart: 1, of which 1 were waited for; matrix products, arithmetic and copies ran while one was open for 0% of the time, Pallas kernels for 0%

commit v1 on v0

--- a/solution.py
+++ b/solution.py
@@ -82,13 +82,16 @@
         noise_re_list.append(noise_prod[:, 0, :, 0, :] + noise_prod[:, 1, :, 1, :])
         noise_im_list.append(noise_prod[:, 0, :, 1, :] - noise_prod[:, 1, :, 0, :])
     low_re, low_im, noise_re, noise_im = lax.psum(
-        (
-            jnp.stack(low_re_list),
-            jnp.stack(low_im_list),
-            jnp.stack(noise_re_list),
-            jnp.stack(noise_im_list),
+        lax.psum(
+            (
+                jnp.stack(low_re_list),
+                jnp.stack(low_im_list),
+                jnp.stack(noise_re_list),
+                jnp.stack(noise_im_list),
+            ),
+            "gx",
         ),
-        ("gx", "gy", "gz"),
+        ("gy", "gz"),
     )
     noise_float = noise_onehot.astype(jnp.float32)
     noise_coef_re = jnp.einsum("gsr,rj->gsj", coef_re, noise_float, precision=EXACT)

time: 340 us -> 343 us (level)
    psum x0 -> x1, waiting for transfers between devices: none -> 197 us  [local(): lax.psum(lax.psum((jnp.stack(low_re_list), jnp.stack(low_im_list), jnp.st...]
    psum x1, waiting for transfers between devices: 268 us -> 74.1 us  [local(): lax.psum((jnp.stack(low_re_list), jnp.stack(low_im_list), jnp.stack(noise...]
  transfers between devices with their start and end apart: 1 -> 2, of which waited for: 1 -> 2; matrix products, arithmetic and copies ran while one was open for 0% -> 0% of each run, Pallas kernels for 0% -> 0%
where the time goes in v1:
time: 343 us
  waiting for transfers between devices  271 us (79%)
  matrix products  39.5 us (12%)
  between operations  14.4 us (4%)
  local copies, waits for them, and re-layouts  11.4 us (3%)
  other arithmetic  6.25 us (2%)
    psum x1, waiting for transfers between devices, local(): lax.psum(lax.psum((jnp.stack(low_re_list), jnp.stack(low_im_list), jnp.st...  197 us
    psum x1, waiting for transfers between devices, local(): lax.psum((jnp.stack(low_re_list), jnp.stack(low_im_list), jnp.stack(noise...  74.1 us
    dot_general x1, matrix products, finish_whole(): jnp.einsum('gtaij,hubji->gtahub', my_gammas, summed, precision=EXACT)  17.5 us
  transfers between devices with their start and end apart: 2, of which 2 were waited for; matrix products, arithmetic and copies ran while one was open for 0% of the time, Pallas kernels for 0%

profile of v1, /device:TPU:2, one launch (start us, length us, event | category | flops | bytes accessed | tf_op | source)
XLA Modules:
  0.0 342.6 jit_solution(10523657598626705709)
XLA Ops:
  7.2 0.0 copy-start.7
  7.2 0.0 all-reduce.7.cloned.1.call-start
  7.2 0.0 copy-start.3
  7.2 3.5 %slice_bitcast_fusion = (bf16[4,2,128,3,512]{4,2,3,1,0:T(8,128)(2,1)S(1)}, bf16[4,2,128,3,512]{4,2,3,1,0:T(8,128)(2,1)S(1)}) fusion(bf16[2,4,2,128,3,512]{5,3,4,2,1,0:T(8,128)(2,1)} %param.7), kind=kLoop, calls=%fused_computation.11 | loop fusion | bytes 12582912 | tf_op jit(solution)/shard_map/squeeze | solution.py:67
  10.7 0.0 copy-done.7
  10.7 1.1 copy-done.3
  11.9 0.7 slice_bitcast_fusion.3
  12.6 0.9 fusion.19
  13.5 1.1 fusion.30
  14.7 1.8 fusion.15
  16.5 0.1 fusion.38
  16.6 0.1 fusion.41
  16.7 1.1 fusion.27
  17.8 1.8 fusion.12
  19.6 0.1 fusion.37
  19.8 0.8 pad_maximum_fusion.2
  20.6 1.5 pad_maximum_fusion
  22.1 0.0 copy-start.8
  22.1 0.0 copy-start.6
  22.1 0.0 copy-start.9
  22.1 0.0 all-reduce.7.cloned.1.call-update
  22.2 0.2 all-reduce.5.cloned.1.call-start
  22.4 74.1 %all-reduce.7.cloned.1.call-done = (f32[2,4,128,64]{2,3,1,0:T(8,128)}, f32[2,4,128,64]{2,3,1,0:T(8,128)}, f32[2,4,4,128,64]{3,4,1,2,0:T(8,128)}, f32[2,4,4,128,64]{3,4,1,2,0:T(8,128)}) async-done(((f32[2,4,128,64]{2,3,1,0:T(8,128)}, f32[2,4,128,64]{2,3,1,0:T(8,128)}, f32[2,4,4,128,64]{3,4,1,2,0:T(8,128)}, f32[2,4,4,128,64]{3,4,1,2,0:T(8,128)}), (f32[2,4,128,64]{2,3,1,0:T(8,128)}, ...) | async-done | bytes 2621456 | tf_op jit(solution)/shard_map/psum | solution.py:85
  96.4 0.0 all-reduce.5.cloned.1.call-update
  96.5 0.0 copy-done.8
  96.5 0.0 copy-done.6
  96.5 0.2 fusion.61
  96.7 0.1 copy.23
  96.8 0.2 fusion.59
  97.1 0.1 copy.25
  97.2 0.0 copy-done.9
  97.2 196.6 %all-reduce.5.cloned.1.call-done = (f32[2,4,128,64]{2,3,1,0:T(8,128)}, f32[2,4,128,64]{2,3,1,0:T(8,128)}, f32[2,4,4,128,64]{3,4,1,2,0:T(8,128)}, f32[2,4,4,128,64]{3,4,1,2,0:T(8,128)}) async-done(((f32[2,4,128,64]{2,3,1,0:T(8,128)}, f32[2,4,128,64]{2,3,1,0:T(8,128)}, f32[2,4,4,128,64]{3,4,1,2,0:T(8,128)}, f32[2,4,4,128,64]{3,4,1,2,0:T(8,128)}), (f32[2,4,128,64]{2,3,1,0:T(8,128)}, ...) | async-done | bytes 2621456 | tf_op jit(solution)/shard_map/psum | solution.py:84
  293.8 0.0 copy-start.2
  293.8 3.3 convolution_bitcast_fusion.2
  297.1 0.0 copy-start.1
  297.2 3.3 convolution_bitcast_fusion
  300.5 0.0 copy-done.2
  300.5 0.0 copy-start.4
  300.5 0.0 copy-start.5
  300.5 2.0 fusion.24
  302.5 0.0 copy-done.1
  302.5 2.0 fusion.26
  304.5 0.0 copy-done.4
  304.5 1.2 fusion.48
  305.7 0.0 copy-done.5
  305.7 1.2 fusion.44
  306.9 1.2 fusion.22
  308.1 1.4 fusion.21
  309.5 2.7 fusion.101
  312.1 0.0 copy-start
  312.1 2.0 copy-done
  314.1 0.2 constant_dynamic-slice_fusion
  314.3 0.2 copy.67
  314.5 17.5 %fusion = f32[2,2,16,2,2,1]{2,1,5,4,3,0:T(2,128)S(1)} fusion(f32[2,2,128,128,1,1]{3,1,2,5,4,0:T(2,128)S(1)} %copy.67, f32[16,2,2,128,128,1]{3,0,4,1,2,5:T(8,128)} %get-tuple-element.18), kind=kOutput, calls=%fused_computation.1 | convolution fusion | flops 50331648 | bytes 4457472 | tf_op jit(solution)/shard_map/gtaij,hubji->gtahub/dot_general | solution.py:42
  332.0 0.2 convolution_bitcast_fusion.4
  332.2 0.6 copy.35
  332.8 2.2 constant_dynamic-slice_fusion.1
  335.0 0.7 copy.34
  (9 shorter events, 0.1 us)
Async XLA Ops:
  7.2 3.6 %copy-start.7 = (s32[64]{0:T(128)S(1)}, s32[64]{0:T(128)}, u32[]{:S(2)}) copy-start(s32[64]{0:T(128)} %param.10) | copy-start | bytes 772
  7.2 89.3 %all-reduce.7.cloned.1.call-start = ((), (), s32[]{:S(2)}) async-start(), calls=%async_computation.1 | async-start | bytes 5242880 | tf_op jit(solution)/shard_map/psum | solution.py:85
  7.2 4.6 %copy-start.3 = (bf16[2,4,2,128,3,512]{5,3,4,2,1,0:T(8,128)(2,1)S(1)}, bf16[2,4,2,128,3,512]{5,3,4,2,1,0:T(8,128)(2,1)}, u32[]{:S(2)}) copy-start(bf16[2,4,2,128,3,512]{5,3,4,2,1,0:T(8,128)(2,1)} %param.6) | copy-start | bytes 18874372
  22.1 74.3 %copy-start.8 = (s32[16,4]{0,1:T(4,128)S(1)}, s32[16,4]{0,1:T(4,128)}, u32[]{:S(2)}) copy-start(s32[16,4]{0,1:T(4,128)} %param.9) | copy-start | bytes 772
  22.1 74.4 %copy-start.6 = (s32[16,4]{0,1:T(4,128)S(1)}, s32[16,4]{0,1:T(4,128)}, u32[]{:S(2)}) copy-start(s32[16,4]{0,1:T(4,128)} %param.8) | copy-start | bytes 772
  22.1 75.1 %copy-start.9 = (s32[4,2]{0,1:T(2,128)S(1)}, s32[4,2]{0,1:T(2,128)}, u32[]{:S(2)}) copy-start(s32[4,2]{0,1:T(2,128)} %param.11) | copy-start | bytes 100
  22.2 271.7 %all-reduce.5.cloned.1.call-start = ((), (), s32[]{:S(2)}) async-start(), calls=%async_computation | async-start | bytes 5242880 | tf_op jit(solution)/shard_map/psum | solution.py:84
  293.8 6.6 %copy-start.2 = (f32[2,4,4,128,64]{3,4,1,2,0:T(8,128)S(1)}, f32[2,4,4,128,64]{3,4,1,2,0:T(8,128)}, u32[]{:S(2)}) copy-start(f32[2,4,4,128,64]{3,4,1,2,0:T(8,128)} %get-tuple-element.8) | copy-start | bytes 3145732
  297.1 5.4 %copy-start.1 = (f32[2,4,4,128,64]{3,4,1,2,0:T(8,128)S(1)}, f32[2,4,4,128,64]{3,4,1,2,0:T(8,128)}, u32[]{:S(2)}) copy-start(f32[2,4,4,128,64]{3,4,1,2,0:T(8,128)} %get-tuple-element.9) | copy-start | bytes 3145732
  300.5 4.0 %copy-start.4 = (f32[2,4,128,64]{2,3,1,0:T(8,128)S(1)}, f32[2,4,128,64]{2,3,1,0:T(8,128)}, u32[]{:S(2)}) copy-start(f32[2,4,128,64]{2,3,1,0:T(8,128)} %get-tuple-element.7) | copy-start | bytes 786436
  300.5 5.2 %copy-start.5 = (f32[2,4,128,64]{2,3,1,0:T(8,128)S(1)}, f32[2,4,128,64]{2,3,1,0:T(8,128)}, u32[]{:S(2)}) copy-start(f32[2,4,128,64]{2,3,1,0:T(8,128)} %get-tuple-element.6) | copy-start | bytes 786436
  312.1 2.0 copy-start
Sparse Core Ops, SparseCore 0:
  22.3 74.1 all-reduce.6
  100.4 193.4 all-reduce.4
